TPU v7x, 32 devices: a whole 2x2x4 slice. The times are simulated.
32 devices in a mesh: ta: 1, gx: 8 (over y, x, core), gy: 4 (over z).
Axes of the slice: x: 2, y: 2, z: 4, core: 2. Of those that a mesh axis runs over, the one named last changes fastest.
Arguments:
- propagator: bfloat16 [1, 2, 4, 3, 4, 3, 64, 4096], P('ta', None, None, None, None, None, 'gx', 'gy'), may hold values from -1.5 to 1.5
- gamma_table: int32 [16, 8], replicated, may hold values from 0 to 3, as said below
Outputs:
- spectrum: float32 [1, 16, 64, 64, 128], P('ta', None, ('gx', 'gy'))
Inputs may be any that keep to these rules, and one draw needn't show every extreme that they name: gamma_table[g, 0:4] is a permutation of 0 to 3, gamma_table[g, 4:8] are powers of i.
All inputs are finite; a program needn't handle non-finite values.
Results may differ from a plain program's by a relative error of at most 0.0061.
Values may be sent and summed in bfloat16 or wider, within the bound.
A program may use at most 192 MiB of HBM per device.

v0:
```python
import functools
import math

import jax
import jax.numpy as jnp
import numpy as np
from jax import lax
from jax.experimental import pallas as pl
from jax.experimental.pallas import tpu as pltpu
from jax.sharding import PartitionSpec as P

LANES = 128
SPINS = 4
COLORS = 3
PAIRED = 2
MESH = pl.DeviceIdType.MESH


def pair_rows():
    rows = []
    for left in range(SPINS):
        for right in range(left, SPINS):
            for i in range(SPINS):
                for j in range(SPINS):
                    if left == right and i > j:
                        continue
                    if left == right and i == j:
                        rows.append((left, i, right, j, 2))
                    else:
                        rows.append((left, i, right, j, 0))
                        rows.append((left, i, right, j, 1))
    return rows


ROWS = pair_rows()
ROW_OF = {row: position for position, row in enumerate(ROWS)}


def dft_tables(length):
    index = np.arange(length)
    angles = (index[:, None] * index[None, :] % length) * (2.0 * math.pi / length)
    norm = 1.0 / math.sqrt(length)
    half = lambda v: (v * norm).astype(jnp.bfloat16).astype(np.float32)
    return half(np.cos(angles)), half(np.sin(angles))


def table_z(extent):
    cosine, sine = dft_tables(extent)
    per_tile = LANES // extent
    same = np.eye(per_tile, dtype=np.float32)
    block = np.zeros((extent, 2, per_tile, 2, per_tile, extent), np.float32)
    for c_out, c_in, values in ((0, 0, cosine), (0, 1, sine), (1, 0, -sine), (1, 1, cosine)):
        block[:, c_out, :, c_in] = np.einsum("zk,ab->kabz", values, same)
    return block.reshape(2 * LANES, 2 * LANES)


def table_y(extent, local_k):
    cosine, sine = dft_tables(extent)
    per_tile = LANES // extent
    groups = extent // per_tile
    block = np.zeros((groups, local_k, 2, per_tile, 2, local_k, 2, extent), np.float32)
    entries = (
        (0, 0, 0, cosine), (0, 0, 1, sine), (0, 1, 0, -sine), (0, 1, 1, cosine),
        (1, 0, 0, -sine), (1, 0, 1, cosine), (1, 1, 0, -cosine), (1, 1, 1, -sine),
    )
    for copy, c_out, c_in, values in entries:
        for k in range(local_k):
            block[:, k, c_in, :, copy, k, c_out] = values.reshape(groups, per_tile, extent)
    return block.reshape(groups * local_k * 2 * per_tile, 2 * local_k * 2 * extent)


def table_x(extent):
    cosine, sine = dft_tables(extent)
    return np.concatenate([cosine.T, sine.T], axis=1)


def folded_weights(table, rows):
    channels = table.shape[0]
    a1, a2, b1, b2, kind = (rows[i : i + 1, :] for i in range(5))

    def pick(spin, base):
        value = jnp.zeros((channels, rows.shape[1]), jnp.int32)
        for s in range(SPINS):
            value = jnp.where(spin == s, table[:, base + s : base + s + 1], value)
        return value

    def term(l1, l2, r1, r2):
        hit = (pick(r1, 0) == l1) & (pick(l2, 0) == r2)
        code = (pick(r1, SPINS) + pick(l2, SPINS)) & 3
        one = jnp.where(hit, 1.0, 0.0)
        real = jnp.where(code == 0, one, jnp.where(code == 2, -one, 0.0))
        imag = jnp.where(code == 1, one, jnp.where(code == 3, -one, 0.0))
        return real, imag

    fore_real, fore_imag = term(a1, a2, b1, b2)
    back_real, back_imag = term(b1, b2, a1, a2)
    sign = jnp.where(kind == 0, 1.0, jnp.where(kind == 1, -1.0, 0.0))
    real = fore_real + sign * back_real
    imag = fore_imag + sign * back_imag
    weight_real = jnp.where(kind == 1, -imag, real)
    weight_imag = jnp.where(kind == 1, real, imag)
    return jnp.concatenate([weight_real, weight_imag], axis=0).astype(jnp.bfloat16)


def component(s1, c1, s2, c2):
    return ((s1 * COLORS + c1) * SPINS + s2) * COLORS + c2


def products(parts, rows_out):
    def put(row, value):
        rows_out[pl.ds(ROW_OF[row] * 8, 8), :] = value

    colors = [(c1, c2) for c1 in range(COLORS) for c2 in range(COLORS)]
    for left in range(SPINS):
        for right in range(left, SPINS):
            for half in ((0, 1), (2, 3)):
                pairs = [(i, j) for i in half for j in range(SPINS) if left != right or i < j]
                diagonal = half if left == right else ()
                sums = {}
                for c1, c2 in colors:
                    at_a = {i: component(left, c1, i, c2) for i in half}
                    at_b = {j: component(right, c1, j, c2) for j in {j for _, j in pairs}}
                    a = {i: (parts[0, n], parts[1, n], parts[2, n]) for i, n in at_a.items()}
                    b = {j: (parts[0, n], parts[2, n], parts[3, n]) for j, n in at_b.items()}
                    for i, j in pairs:
                        new = (a[i][2] * b[j][0], a[i][0] * b[j][1], a[i][1] * b[j][2])
                        old = sums.get((i, j))
                        sums[i, j] = new if old is None else tuple(o + v for o, v in zip(old, new))
                    for i in diagonal:
                        new = a[i][0] * a[i][0] + a[i][1] * a[i][1]
                        old = sums.get(i)
                        sums[i] = new if old is None else old + new
                for i, j in pairs:
                    first, second, third = sums[i, j]
                    put((left, i, right, j, 0), first - third)
                    put((left, i, right, j, 1), first - second)
                for i in diagonal:
                    put((left, i, right, i, 2), sums[i])


def front_kernel(
    grid_x, grid_y, prop, table_in, rows_in, dft_in, out,
    staged, parts, prod, dens, weights, sent, table, rows, dft,
    load_sems, small_sems, send_sem, recv_sem,
):
    devices, steps = out.shape[0], out.shape[1]
    tiles = staged.shape[0]
    entries = parts.shape[1]
    channels = table.shape[1]

    def load(t):
        return pltpu.make_async_copy(
            prop.at[:, :, pl.ds(t * LANES, LANES)], staged.at[t], load_sems.at[t]
        )

    me_x, me_y = lax.axis_index("gx"), lax.axis_index("gy")
    me = me_x * grid_y + me_y
    if grid_y == 4:
        columns_y = [lax.rem(me_y + 2, 4), me_y + 1 - 2 * lax.rem(me_y, 2), 3 - me_y]
    else:
        columns_y = [lax.rem(me_y + i, grid_y) for i in range(1, grid_y)]

    def for_others(act):
        @pl.loop(1, grid_x)
        def _(i):
            to_x = lax.rem(me_x + i, grid_x)
            for to_y in columns_y:
                act(to_x, to_y)
            act(to_x, me_y)

        for to_y in columns_y:
            act(me_x, to_y)

    small = [
        pltpu.make_async_copy(source, target, small_sems.at[n])
        for n, (source, target) in enumerate(((table_in, table), (rows_in, rows), (dft_in, dft)))
    ]
    load(0).start()
    for copy in small:
        copy.start()
    for t in range(1, tiles):
        load(t).start()
    barrier = pltpu.get_barrier_semaphore()
    for_others(
        lambda x, y: pl.semaphore_signal(
            barrier, inc=1, device_id={"gx": x, "gy": y}, device_id_type=MESH
        )
    )
    small[0].wait()
    small[1].wait()
    weights[...] = folded_weights(jnp.transpose(table[...]), rows[...])
    small[2].wait()
    pl.semaphore_wait(barrier, grid_x * grid_y - 1)

    @pl.loop(0, steps)
    def _(k):
        @pl.loop(0, PAIRED)
        def _(half):
            t = k * PAIRED + half
            pltpu.make_async_copy(
                prop.at[:, :, pl.ds(0, LANES)], staged.at[t], load_sems.at[t]
            ).wait()
            real = staged[t, 0:entries].astype(jnp.float32)
            parts[0] = real
            imag = staged[t, entries : 2 * entries].astype(jnp.float32)
            parts[1] = imag
            parts[2] = real + imag
            parts[3] = real - imag
            products(parts, prod)
            for x in range(8):
                columns = prod[pl.ds(x, len(ROWS), stride=8), :].astype(jnp.bfloat16)
                value = jnp.dot(weights[...], columns, preferred_element_type=jnp.float32)
                dens[half, 0, pl.ds(x, channels, stride=8), :] = value[:channels]
                dens[half, 1, pl.ds(x, channels, stride=8), :] = value[channels:]

        pieces = []
        for half in range(PAIRED):
            left = jnp.concatenate([dens[half, 0], dens[half, 1]], axis=1).astype(jnp.bfloat16)
            value = lax.dot_general(
                dft[...], left, (((1,), (1,)), ((), ())), preferred_element_type=jnp.float32
            )
            pieces.append(value.reshape(devices, 2 * LANES // devices, LANES))
        block = jnp.concatenate(pieces, axis=1).astype(jnp.bfloat16)
        sent[:, k] = block
        pltpu.make_async_copy(sent.at[me, k], out.at[me, k], recv_sem).start()
        for_others(
            lambda x, y: pltpu.make_async_remote_copy(
                src_ref=sent.at[x * grid_y + y, k], dst_ref=out.at[me, k],
                send_sem=send_sem, recv_sem=recv_sem,
                device_id={"gx": x, "gy": y}, device_id_type=MESH,
            ).start()
        )

    pltpu.make_async_copy(out, out, recv_sem).wait()
    rest = sent.at[pl.ds(0, devices - 1)]
    pltpu.make_async_copy(rest, rest, send_sem).wait()


def front(prop, gamma_table, devices, grid_y, extent):
    entries, rows_x, sites = prop.shape
    tiles = sites // LANES
    steps = tiles // PAIRED
    height = 2 * LANES // devices * PAIRED
    channels = gamma_table.shape[0]
    rows = np.zeros((8, len(ROWS)), np.int32)
    rows[:5] = np.array(ROWS, np.int32).T
    return pl.pallas_call(
        functools.partial(front_kernel, devices // grid_y, grid_y),
        out_shape=jax.ShapeDtypeStruct((devices, steps, height, LANES), jnp.bfloat16),
        in_specs=[pl.BlockSpec(memory_space=pl.ANY)] * 4,
        out_specs=pl.BlockSpec(memory_space=pl.ANY),
        scratch_shapes=[
            pltpu.VMEM((tiles, entries, rows_x, LANES), jnp.bfloat16),
            pltpu.VMEM((4, entries // 2, rows_x, LANES), jnp.float32),
            pltpu.VMEM((len(ROWS) * rows_x, LANES), jnp.float32),
            pltpu.VMEM((PAIRED, 2, channels * rows_x, LANES), jnp.float32),
            pltpu.VMEM((2 * channels, len(ROWS)), jnp.bfloat16),
            pltpu.VMEM((devices, steps, height, LANES), jnp.bfloat16),
            pltpu.VMEM(gamma_table.shape[::-1], jnp.int32),
            pltpu.VMEM(rows.shape, jnp.int32),
            pltpu.VMEM((2 * LANES, 2 * LANES), jnp.bfloat16),
            pltpu.SemaphoreType.DMA((tiles,)),
            pltpu.SemaphoreType.DMA((3,)),
            pltpu.SemaphoreType.DMA,
            pltpu.SemaphoreType.DMA,
        ],
        compiler_params=pltpu.CompilerParams(
            vmem_limit_bytes=62 * 1024 * 1024, collective_id=0, has_side_effects=True
        ),
    )(prop, gamma_table.T, jnp.asarray(rows), jnp.asarray(table_z(extent), jnp.bfloat16))


def back_kernel(blocks, along_y, along_x, out, mid):
    grid_x, _, width = blocks.shape
    channels, local_k, extent, lanes = out.shape
    rows_x = width // channels
    cols = local_k * lanes
    for gx in range(grid_x):
        mid[gx] = lax.dot_general(
            blocks[gx], along_y[...], (((0,), (0,)), ((), ())), preferred_element_type=jnp.float32
        )
    for g in range(channels):
        value = mid[:, g * rows_x : (g + 1) * rows_x, :].reshape(grid_x * rows_x, 2 * cols)
        value = value.astype(jnp.bfloat16)
        stacked = jnp.concatenate([value[:, :cols], value[:, cols:]], axis=0)
        result = jnp.dot(along_x[...], stacked, preferred_element_type=jnp.float32)
        for k in range(local_k):
            out[g, k] = result[:, k * lanes : (k + 1) * lanes]


def back(blocks, channels, extent, local_k):
    grid_x, _, width = blocks.shape
    vmem = pl.BlockSpec(memory_space=pltpu.VMEM)
    return pl.pallas_call(
        back_kernel,
        out_shape=jax.ShapeDtypeStruct((channels, local_k, extent, 2 * extent), jnp.float32),
        in_specs=[vmem] * 3,
        out_specs=vmem,
        scratch_shapes=[pltpu.VMEM((grid_x, width, 4 * local_k * extent), jnp.float32)],
        compiler_params=pltpu.CompilerParams(vmem_limit_bytes=24 * 1024 * 1024),
    )(
        blocks,
        jnp.asarray(table_y(extent, local_k), jnp.bfloat16),
        jnp.asarray(table_x(extent), jnp.bfloat16),
    )


def body(propagator, gamma_table):
    slices, rows_x, sites = propagator.shape[0], propagator.shape[-2], propagator.shape[-1]
    grid_x, grid_y = lax.axis_size("gx"), lax.axis_size("gy")
    devices = grid_x * grid_y
    extent = grid_x * rows_x
    channels = gamma_table.shape[0]
    local_k = extent // devices
    results = []
    for t in range(slices):
        prop = propagator[t].reshape(-1, rows_x, sites)
        blocks = front(prop, gamma_table, devices, grid_y, extent)
        blocks = blocks.reshape(grid_x, -1, LANES)
        results.append(back(blocks, channels, extent, local_k))
    return jnp.stack(results)


def solution(mesh):
    return jax.shard_map(
        body,
        mesh=mesh,
        in_specs=(P("ta", None, None, None, None, None, "gx", "gy"), P()),
        out_specs=P("ta", None, ("gx", "gy"), None, None),
        check_vma=False,
    )
```

profile of v0, /device:TPU:0, one launch (start us, length us, event | category | flops | bytes accessed | tf_op | source)
XLA Modules:
  0.0 27.2 jit_solution(12451069999415516251)
XLA Ops:
  0.0 0.0 copy-start.2
  0.0 0.0 copy-start.1
  0.0 24.4 %shard_map.64 = bf16[32,4,16,128]{3,2,1,0:T(8,128)(2,1)} custom-call(bf16[288,8,1024]{2,1,0:T(8,128)(2,1)} %bitcast.5, s32[8,16]{1,0:T(8,128)} %bitcast.6, s32[8,256]{1,0:T(8,128)} %constant.8.clone.rows_in, bf16[256,256]{1,0:T(8,128)(2,1)} %constant.9.clone.dft_in), custom_call_target="tpu_custom_call" | custom-call | tf_op jit(solution)/shard_map/pallas_call | solution.py:247
  24.4 0.0 copy-done.2
  24.4 0.0 copy-done.1
  24.4 0.0 copy-start
  24.5 1.0 %copy-done = bf16[32,4,16,128]{3,2,1,0:T(8,128)(2,1)S(1)} copy-done((bf16[32,4,16,128]{3,2,1,0:T(8,128)(2,1)S(1)}, bf16[32,4,16,128]{3,2,1,0:T(8,128)(2,1)}, u32[]{:S(2)}) %copy-start) | copy-done | bytes 524312
  25.5 1.7 %shard_map.65 = f32[16,2,64,128]{3,2,1,0:T(8,128)} custom-call(bf16[8,256,128]{2,1,0:T(8,128)(2,1)S(1)} %bitcast.4, bf16[256,512]{1,0:T(8,128)(2,1)S(1)} %copy-done.1, bf16[64,128]{1,0:T(8,128)(2,1)S(1)} %copy-done.2), custom_call_target="tpu_custom_call" | custom-call | tf_op jit(solution)/shard_map/pallas_call | solution.py:294
Async XLA Ops:
  0.0 24.4 %copy-start.2 = (bf16[64,128]{1,0:T(8,128)(2,1)S(1)}, bf16[64,128]{1,0:T(8,128)(2,1)}, u32[]{:S(2)}) copy-start(bf16[64,128]{1,0:T(8,128)(2,1)} %constant.11.clone.along_x) | copy-start | bytes 49156
  0.0 24.4 %copy-start.1 = (bf16[256,512]{1,0:T(8,128)(2,1)S(1)}, bf16[256,512]{1,0:T(8,128)(2,1)}, u32[]{:S(2)}) copy-start(bf16[256,512]{1,0:T(8,128)(2,1)} %constant.10.clone.along_y) | copy-start | bytes 786436
  24.4 1.0 %copy-start = (bf16[32,4,16,128]{3,2,1,0:T(8,128)(2,1)S(1)}, bf16[32,4,16,128]{3,2,1,0:T(8,128)(2,1)}, u32[]{:S(2)}) copy-start(bf16[32,4,16,128]{3,2,1,0:T(8,128)(2,1)} %shard_map.64) | copy-start | bytes 1572868
where the time goes:
time: 27.3 us; the launch traced here: 27.2 us
  Pallas kernels  26.1 us (96%)
  local copies, waits for them, and re-layouts  1.04 us (4%)
    pallas_call x1, Pallas kernels, front(): pl.pallas_call(functools.partial(front_kernel, devices // grid_y, grid_y)...  24.4 us
    pallas_call x1, Pallas kernels, back(): pl.pallas_call(back_kernel, out_shape=jax.ShapeDtypeStruct((channels, loc...  1.7 us
    unnamed x6, local copies, waits for them, and re-layouts  1.04 us

commit v1 on v0

--- a/solution.py
+++ b/solution.py
@@ -12,6 +12,7 @@
 LANES = 128
 SPINS = 4
 COLORS = 3
+PITCH = 8
 PAIRED = 2
 MESH = pl.DeviceIdType.MESH
 
@@ -107,68 +108,95 @@
 
 
 def products(parts, rows_out):
+    entries = parts.shape[0] // 2
+    pitch = rows_out.shape[1] // parts.shape[1]
+
     def put(row, value):
-        rows_out[pl.ds(ROW_OF[row] * 8, 8), :] = value
-
-    colors = [(c1, c2) for c1 in range(COLORS) for c2 in range(COLORS)]
+        value = value.astype(jnp.float32)
+        for h in range(PAIRED):
+            rows_out[h, pl.ds(ROW_OF[row], parts.shape[1], stride=pitch), :] = (
+                value[:, h * LANES : (h + 1) * LANES]
+            )
+
+    def group(terms):
+        total = terms[0]
+        for term in terms[1:]:
+            total = total + term
+        return total
+
     for left in range(SPINS):
         for right in range(left, SPINS):
             for half in ((0, 1), (2, 3)):
                 pairs = [(i, j) for i in half for j in range(SPINS) if left != right or i < j]
                 diagonal = half if left == right else ()
                 sums = {}
-                for c1, c2 in colors:
-                    at_a = {i: component(left, c1, i, c2) for i in half}
-                    at_b = {j: component(right, c1, j, c2) for j in {j for _, j in pairs}}
-                    a = {i: (parts[0, n], parts[1, n], parts[2, n]) for i, n in at_a.items()}
-                    b = {j: (parts[0, n], parts[2, n], parts[3, n]) for j, n in at_b.items()}
-                    for i, j in pairs:
-                        new = (a[i][2] * b[j][0], a[i][0] * b[j][1], a[i][1] * b[j][2])
-                        old = sums.get((i, j))
-                        sums[i, j] = new if old is None else tuple(o + v for o, v in zip(old, new))
-                    for i in diagonal:
-                        new = a[i][0] * a[i][0] + a[i][1] * a[i][1]
-                        old = sums.get(i)
-                        sums[i] = new if old is None else old + new
+                for c1 in range(COLORS):
+                    part = {}
+                    for c2 in range(COLORS):
+                        at_a = {i: component(left, c1, i, c2) for i in half}
+                        at_b = {j: component(right, c1, j, c2) for j in sorted({j for _, j in pairs})}
+                        a = {i: (parts[n], parts[entries + n]) for i, n in at_a.items()}
+                        b = {j: (parts[n], parts[entries + n]) for j, n in at_b.items()}
+                        for i, j in pairs:
+                            re = a[i][0] * b[j][0] + a[i][1] * b[j][1]
+                            im = a[i][1] * b[j][0] - a[i][0] * b[j][1]
+                            old = part.get((i, j))
+                            part[i, j] = (re, im) if old is None else (old[0] + re, old[1] + im)
+                        for i in diagonal:
+                            re = a[i][0] * a[i][0] + a[i][1] * a[i][1]
+                            old = part.get(i)
+                            part[i] = (re,) if old is None else (old[0] + re,)
+                    for key, values in part.items():
+                        values = tuple(v.astype(jnp.float32) for v in values)
+                        old = sums.get(key)
+                        sums[key] = values if old is None else tuple(o + v for o, v in zip(old, values))
                 for i, j in pairs:
-                    first, second, third = sums[i, j]
-                    put((left, i, right, j, 0), first - third)
-                    put((left, i, right, j, 1), first - second)
+                    put((left, i, right, j, 0), sums[i, j][0])
+                    put((left, i, right, j, 1), sums[i, j][1])
                 for i in diagonal:
-                    put((left, i, right, i, 2), sums[i])
+                    put((left, i, right, i, 2), sums[i][0])
 
 
 def front_kernel(
     grid_x, grid_y, prop, table_in, rows_in, dft_in, out,
-    staged, parts, prod, dens, weights, sent, table, rows, dft,
+    staged, prod, dens, weights, sent, table, rows, dft,
     load_sems, small_sems, send_sem, recv_sem,
 ):
-    devices, steps = out.shape[0], out.shape[1]
+    devices = out.shape[0]
     tiles = staged.shape[0]
-    entries = parts.shape[1]
+    rows_x, width = staged.shape[2:]
+    pitch = prod.shape[1] // rows_x
     channels = table.shape[1]
 
     def load(t):
         return pltpu.make_async_copy(
-            prop.at[:, :, pl.ds(t * LANES, LANES)], staged.at[t], load_sems.at[t]
+            prop.at[:, :, pl.ds(t * width, width)], staged.at[t], load_sems.at[t]
         )
 
     me_x, me_y = lax.axis_index("gx"), lax.axis_index("gy")
     me = me_x * grid_y + me_y
     if grid_y == 4:
-        columns_y = [lax.rem(me_y + 2, 4), me_y + 1 - 2 * lax.rem(me_y, 2), 3 - me_y]
+        low = lax.rem(me_y, 2)
+        other = 2 - (me_y - low)
+        far, near = [other + low, other + 1 - low], [me_y + 1 - 2 * low]
     else:
-        columns_y = [lax.rem(me_y + i, grid_y) for i in range(1, grid_y)]
+        far, near = [lax.rem(me_y + i, grid_y) for i in range(1, grid_y)], []
 
     def for_others(act):
+        @pl.loop(0, grid_x)
+        def _(i):
+            to_x = lax.rem(me_x + i, grid_x)
+            for to_y in far:
+                act(to_x, to_y)
+
         @pl.loop(1, grid_x)
         def _(i):
             to_x = lax.rem(me_x + i, grid_x)
-            for to_y in columns_y:
+            for to_y in near:
                 act(to_x, to_y)
             act(to_x, me_y)
 
-        for to_y in columns_y:
+        for to_y in near:
             act(me_x, to_y)
 
     small = [
@@ -190,72 +218,71 @@
     small[1].wait()
     weights[...] = folded_weights(jnp.transpose(table[...]), rows[...])
     small[2].wait()
-    pl.semaphore_wait(barrier, grid_x * grid_y - 1)
-
-    @pl.loop(0, steps)
-    def _(k):
-        @pl.loop(0, PAIRED)
-        def _(half):
-            t = k * PAIRED + half
-            pltpu.make_async_copy(
-                prop.at[:, :, pl.ds(0, LANES)], staged.at[t], load_sems.at[t]
-            ).wait()
-            real = staged[t, 0:entries].astype(jnp.float32)
-            parts[0] = real
-            imag = staged[t, entries : 2 * entries].astype(jnp.float32)
-            parts[1] = imag
-            parts[2] = real + imag
-            parts[3] = real - imag
-            products(parts, prod)
-            for x in range(8):
-                columns = prod[pl.ds(x, len(ROWS), stride=8), :].astype(jnp.bfloat16)
+
+    @pl.loop(0, tiles)
+    def _(t):
+        load(t).wait()
+        products(staged.at[t], prod)
+        for h in range(PAIRED):
+            for x in range(rows_x):
+                columns = prod[h, pl.ds(x * pitch, len(ROWS)), :].astype(jnp.bfloat16)
                 value = jnp.dot(weights[...], columns, preferred_element_type=jnp.float32)
-                dens[half, 0, pl.ds(x, channels, stride=8), :] = value[:channels]
-                dens[half, 1, pl.ds(x, channels, stride=8), :] = value[channels:]
-
-        pieces = []
-        for half in range(PAIRED):
-            left = jnp.concatenate([dens[half, 0], dens[half, 1]], axis=1).astype(jnp.bfloat16)
-            value = lax.dot_general(
-                dft[...], left, (((1,), (1,)), ((), ())), preferred_element_type=jnp.float32
-            )
-            pieces.append(value.reshape(devices, 2 * LANES // devices, LANES))
-        block = jnp.concatenate(pieces, axis=1).astype(jnp.bfloat16)
-        sent[:, k] = block
-        pltpu.make_async_copy(sent.at[me, k], out.at[me, k], recv_sem).start()
+                dens[h, 0, pl.ds(x, channels, stride=rows_x), :] = value[:channels]
+                dens[h, 1, pl.ds(x, channels, stride=rows_x), :] = value[channels:]
+        left = jnp.concatenate(
+            [jnp.concatenate([dens[h, 0], dens[h, 1]], axis=1) for h in range(PAIRED)], axis=0
+        ).astype(jnp.bfloat16)
+        value = lax.dot_general(
+            dft[...], left, (((1,), (1,)), ((), ())), preferred_element_type=jnp.float32
+        )
+        pieces = [
+            value[:, h * LANES : (h + 1) * LANES].reshape(devices, 2 * LANES // devices, LANES)
+            for h in range(PAIRED)
+        ]
+        sent[:, t] = jnp.concatenate(pieces, axis=1).astype(jnp.bfloat16)
+        out[me, t] = sent[me, t]
+
+        @pl.when(t == 0)
+        def _():
+            pl.semaphore_wait(barrier, grid_x * grid_y - 1)
+
         for_others(
             lambda x, y: pltpu.make_async_remote_copy(
-                src_ref=sent.at[x * grid_y + y, k], dst_ref=out.at[me, k],
+                src_ref=sent.at[x * grid_y + y, t], dst_ref=out.at[me, t],
                 send_sem=send_sem, recv_sem=recv_sem,
                 device_id={"gx": x, "gy": y}, device_id_type=MESH,
             ).start()
         )
 
-    pltpu.make_async_copy(out, out, recv_sem).wait()
     rest = sent.at[pl.ds(0, devices - 1)]
+    pltpu.make_async_copy(rest, rest, recv_sem).wait()
     pltpu.make_async_copy(rest, rest, send_sem).wait()
 
 
 def front(prop, gamma_table, devices, grid_y, extent):
     entries, rows_x, sites = prop.shape
-    tiles = sites // LANES
-    steps = tiles // PAIRED
+    tiles = sites // (LANES * PAIRED)
     height = 2 * LANES // devices * PAIRED
     channels = gamma_table.shape[0]
     rows = np.zeros((8, len(ROWS)), np.int32)
     rows[:5] = np.array(ROWS, np.int32).T
+    pinned = [
+        pltpu.with_memory_space_constraint(array, pltpu.HBM)
+        for array in (
+            prop, gamma_table.T, jnp.asarray(rows), jnp.asarray(table_z(extent), jnp.bfloat16)
+        )
+    ]
     return pl.pallas_call(
         functools.partial(front_kernel, devices // grid_y, grid_y),
-        out_shape=jax.ShapeDtypeStruct((devices, steps, height, LANES), jnp.bfloat16),
-        in_specs=[pl.BlockSpec(memory_space=pl.ANY)] * 4,
-        out_specs=pl.BlockSpec(memory_space=pl.ANY),
+        out_shape=pltpu.VMEM((devices, tiles, height, LANES), jnp.bfloat16),
+        in_specs=[pl.BlockSpec(memory_space=pltpu.HBM)] * 4,
+        out_specs=pl.BlockSpec(memory_space=pltpu.VMEM),
         scratch_shapes=[
-            pltpu.VMEM((tiles, entries, rows_x, LANES), jnp.bfloat16),
-            pltpu.VMEM((4, entries // 2, rows_x, LANES), jnp.float32),
-            pltpu.VMEM((len(ROWS) * rows_x, LANES), jnp.float32),
+            pltpu.VMEM((tiles, entries, rows_x, PAIRED * LANES), jnp.bfloat16),
+            pltpu.VMEM((PAIRED, (len(ROWS) + PITCH) * rows_x, LANES), jnp.float32),
             pltpu.VMEM((PAIRED, 2, channels * rows_x, LANES), jnp.float32),
             pltpu.VMEM((2 * channels, len(ROWS)), jnp.bfloat16),
-            pltpu.VMEM((devices, steps, height, LANES), jnp.bfloat16),
+            pltpu.VMEM((devices, tiles, height, LANES), jnp.bfloat16),
             pltpu.VMEM(gamma_table.shape[::-1], jnp.int32),
             pltpu.VMEM(rows.shape, jnp.int32),
             pltpu.VMEM((2 * LANES, 2 * LANES), jnp.bfloat16),
@@ -265,9 +292,9 @@
             pltpu.SemaphoreType.DMA,
         ],
         compiler_params=pltpu.CompilerParams(
-            vmem_limit_bytes=62 * 1024 * 1024, collective_id=0, has_side_effects=True
+            vmem_limit_bytes=60 * 1024 * 1024, collective_id=0, has_side_effects=True
         ),
-    )(prop, gamma_table.T, jnp.asarray(rows), jnp.asarray(table_z(extent), jnp.bfloat16))
+    )(*pinned)
 
 
 def back_kernel(blocks, along_y, along_x, out, mid):

time: 27.3 us -> 23.6 us (0.86)
  Pallas kernels: 26.1 us -> 23.4 us
  local copies, waits for them, and re-layouts: 1.04 us -> 0.01 us
    pallas_call x1, Pallas kernels: 24.4 us -> 21.7 us  [front(): pl.pallas_call(functools.partial(front_kernel, devices // grid_y, grid_y)...]
    unnamed x6 -> x4, local copies, waits for them, and re-layouts: 1.04 us -> 0.01 us
where the time goes in v1:
time: 23.6 us; the launch traced here: 23.4 us
  Pallas kernels  23.4 us (99%)
    pallas_call x1, Pallas kernels, front(): pl.pallas_call(functools.partial(front_kernel, devices // grid_y, grid_y)...  21.7 us
    pallas_call x1, Pallas kernels, back(): pl.pallas_call(back_kernel, out_shape=jax.ShapeDtypeStruct((channels, loc...  1.7 us

profile of v1, /device:TPU:0, one launch (start us, length us, event | category | flops | bytes accessed | tf_op | source)
XLA Modules:
  0.0 23.4 jit_solution(109904170667455737)
XLA Ops:
  0.0 0.0 copy-start.1
  0.0 0.0 copy-start
  0.0 21.7 %shard_map.64 = bf16[32,4,16,128]{3,2,1,0:T(8,128)(2,1)S(1)} custom-call(bf16[288,8,1024]{2,1,0:T(8,128)(2,1)} %bitcast.5, s32[8,16]{1,0:T(8,128)} %bitcast.6, s32[8,256]{1,0:T(8,128)} %constant.8.clone.rows_in, bf16[256,256]{1,0:T(8,128)(2,1)} %constant.9.clone.dft_in), custom_call_target="tpu_custom_call" | custom-call | tf_op jit(solution)/shard_map/pallas_call | solution.py:275
  21.7 0.0 copy-done.1
  21.7 0.0 copy-done
  21.7 1.7 %shard_map.65 = f32[16,2,64,128]{3,2,1,0:T(8,128)} custom-call(bf16[8,256,128]{2,1,0:T(8,128)(2,1)S(1)} %bitcast.4, bf16[256,512]{1,0:T(8,128)(2,1)S(1)} %copy-done, bf16[64,128]{1,0:T(8,128)(2,1)S(1)} %copy-done.1), custom_call_target="tpu_custom_call" | custom-call | tf_op jit(solution)/shard_map/pallas_call | solution.py:321
Async XLA Ops:
  0.0 21.7 %copy-start.1 = (bf16[64,128]{1,0:T(8,128)(2,1)S(1)}, bf16[64,128]{1,0:T(8,128)(2,1)}, u32[]{:S(2)}) copy-start(bf16[64,128]{1,0:T(8,128)(2,1)} %constant.11.clone.along_x) | copy-start | bytes 49156
  0.0 21.7 %copy-start = (bf16[256,512]{1,0:T(8,128)(2,1)S(1)}, bf16[256,512]{1,0:T(8,128)(2,1)}, u32[]{:S(2)}) copy-start(bf16[256,512]{1,0:T(8,128)(2,1)} %constant.10.clone.along_y) | copy-start | bytes 786436

commit v2 on v1

--- a/solution.py
+++ b/solution.py
@@ -104,28 +104,26 @@
 
 
 def component(s1, c1, s2, c2):
-    return ((s1 * COLORS + c1) * SPINS + s2) * COLORS + c2
-
-
-def products(parts, rows_out):
-    entries = parts.shape[0] // 2
-    pitch = rows_out.shape[1] // parts.shape[1]
+    return s1, (c1 * SPINS + s2) * COLORS + c2
+
+
+def products(parts, first, last, rows_out, ready=None):
+    rows_x = parts.shape[-2]
+    pitch = rows_out.shape[1] // rows_x
 
     def put(row, value):
         value = value.astype(jnp.float32)
+        place = pl.ds(ROW_OF[row] - first, rows_x, stride=pitch)
         for h in range(PAIRED):
-            rows_out[h, pl.ds(ROW_OF[row], parts.shape[1], stride=pitch), :] = (
-                value[:, h * LANES : (h + 1) * LANES]
-            )
-
-    def group(terms):
-        total = terms[0]
-        for term in terms[1:]:
-            total = total + term
-        return total
+            rows_out[h, place, :] = value[:, h * LANES : (h + 1) * LANES]
 
     for left in range(SPINS):
         for right in range(left, SPINS):
+            at = [position for row, position in ROW_OF.items() if row[::2][:2] == (left, right)]
+            if not first <= at[0] < last:
+                continue
+            if ready and left == 0:
+                ready(right)
             for half in ((0, 1), (2, 3)):
                 pairs = [(i, j) for i in half for j in range(SPINS) if left != right or i < j]
                 diagonal = half if left == right else ()
@@ -134,20 +132,20 @@
                     part = {}
                     for c2 in range(COLORS):
                         at_a = {i: component(left, c1, i, c2) for i in half}
-                        at_b = {j: component(right, c1, j, c2) for j in sorted({j for _, j in pairs})}
-                        a = {i: (parts[n], parts[entries + n]) for i, n in at_a.items()}
-                        b = {j: (parts[n], parts[entries + n]) for j, n in at_b.items()}
+                        at_b = {j: component(right, c1, j, c2) for _, j in pairs}
+                        a = {i: (parts[0, *n], parts[1, *n]) for i, n in at_a.items()}
+                        b = {j: (parts[0, *n], parts[1, *n]) for j, n in at_b.items()}
                         for i, j in pairs:
                             re = a[i][0] * b[j][0] + a[i][1] * b[j][1]
                             im = a[i][1] * b[j][0] - a[i][0] * b[j][1]
                             old = part.get((i, j))
                             part[i, j] = (re, im) if old is None else (old[0] + re, old[1] + im)
                         for i in diagonal:
-                            re = a[i][0] * a[i][0] + a[i][1] * a[i][1]
+                            wide = tuple(v.astype(jnp.float32) for v in a[i])
+                            re = wide[0] * wide[0] + wide[1] * wide[1]
                             old = part.get(i)
                             part[i] = (re,) if old is None else (old[0] + re,)
                     for key, values in part.items():
-                        values = tuple(v.astype(jnp.float32) for v in values)
                         old = sums.get(key)
                         sums[key] = values if old is None else tuple(o + v for o, v in zip(old, values))
                 for i, j in pairs:
@@ -159,18 +157,24 @@
 
 def front_kernel(
     grid_x, grid_y, prop, table_in, rows_in, dft_in, out,
-    staged, prod, dens, weights, sent, table, rows, dft,
-    load_sems, small_sems, send_sem, recv_sem,
+    staged, upper, lower, part, dens, weights, sent, table, rows, dft,
+    load_sems, spin_sems, small_sems, send_sem, recv_sem,
 ):
     devices = out.shape[0]
     tiles = staged.shape[0]
-    rows_x, width = staged.shape[2:]
-    pitch = prod.shape[1] // rows_x
+    rows_x, width = staged.shape[-2:]
+    pitch = upper.shape[1] // rows_x
+    middle = weights.shape[1] // 2
     channels = table.shape[1]
 
     def load(t):
         return pltpu.make_async_copy(
-            prop.at[:, :, pl.ds(t * width, width)], staged.at[t], load_sems.at[t]
+            prop.at[:, :, :, :, pl.ds(t * width, width)], staged.at[t], load_sems.at[t]
+        )
+
+    def load_spin(spin):
+        return pltpu.make_async_copy(
+            prop.at[:, spin, :, :, pl.ds(0, width)], staged.at[0, :, spin], spin_sems.at[spin]
         )
 
     me_x, me_y = lax.axis_index("gx"), lax.axis_index("gy")
@@ -178,57 +182,66 @@
     if grid_y == 4:
         low = lax.rem(me_y, 2)
         other = 2 - (me_y - low)
-        far, near = [other + low, other + 1 - low], [me_y + 1 - 2 * low]
+        far, near = [other, other + 1], [me_y + 1 - 2 * low]
     else:
         far, near = [lax.rem(me_y + i, grid_y) for i in range(1, grid_y)], []
 
-    def for_others(act):
+    urgent, lazy = far[: len(far) // 2], far[len(far) // 2 :]
+    every = tuple(range(grid_x))
+
+    def targets(columns, own):
+        for i in every[own:]:
+            for to_y in columns:
+                yield (lax.rem(me_x + i, grid_x) if own else jnp.int32(i)), to_y
+
+    def signal_all():
         @pl.loop(0, grid_x)
         def _(i):
-            to_x = lax.rem(me_x + i, grid_x)
-            for to_y in far:
-                act(to_x, to_y)
+            for to_y in far + near:
+                signal(i, to_y)
 
         @pl.loop(1, grid_x)
         def _(i):
-            to_x = lax.rem(me_x + i, grid_x)
-            for to_y in near:
-                act(to_x, to_y)
-            act(to_x, me_y)
-
-        for to_y in near:
-            act(me_x, to_y)
+            signal(lax.rem(me_x + i, grid_x), me_y)
+
+    def signal(x, y):
+        pl.semaphore_signal(
+            barrier, inc=1, device_id={"gx": x, "gy": y}, device_id_type=MESH
+        )
 
     small = [
         pltpu.make_async_copy(source, target, small_sems.at[n])
         for n, (source, target) in enumerate(((table_in, table), (rows_in, rows), (dft_in, dft)))
     ]
-    load(0).start()
-    for copy in small:
-        copy.start()
-    for t in range(1, tiles):
-        load(t).start()
+    load_spin(0).start()
+    small[0].start()
+    small[1].start()
+    for spin in range(1, SPINS):
+        load_spin(spin).start()
+    small[2].start()
     barrier = pltpu.get_barrier_semaphore()
-    for_others(
-        lambda x, y: pl.semaphore_signal(
-            barrier, inc=1, device_id={"gx": x, "gy": y}, device_id_type=MESH
-        )
-    )
-    small[0].wait()
-    small[1].wait()
-    weights[...] = folded_weights(jnp.transpose(table[...]), rows[...])
-    small[2].wait()
-
-    @pl.loop(0, tiles)
-    def _(t):
-        load(t).wait()
-        products(staged.at[t], prod)
-        for h in range(PAIRED):
-            for x in range(rows_x):
-                columns = prod[h, pl.ds(x * pitch, len(ROWS)), :].astype(jnp.bfloat16)
-                value = jnp.dot(weights[...], columns, preferred_element_type=jnp.float32)
-                dens[h, 0, pl.ds(x, channels, stride=rows_x), :] = value[:channels]
-                dens[h, 1, pl.ds(x, channels, stride=rows_x), :] = value[channels:]
+    signal_all()
+    slots = [(h, x) for h in range(PAIRED) for x in range(rows_x)]
+
+    def first_products(t, ready=None):
+        products(staged.at[t], 0, middle, upper, ready)
+
+    def second_products(t):
+        for h, x in slots:
+            columns = upper[h, pl.ds(x * pitch, middle), :].astype(jnp.bfloat16)
+            part[h, x] = jnp.dot(
+                weights[:, :middle], columns, preferred_element_type=jnp.float32
+            )
+        products(staged.at[t], middle, 2 * middle, lower)
+
+    def finish(t, slot):
+        for h, x in slots:
+            columns = lower[h, pl.ds(x * pitch, middle), :].astype(jnp.bfloat16)
+            value = part[h, x] + jnp.dot(
+                weights[:, middle:], columns, preferred_element_type=jnp.float32
+            )
+            dens[h, 0, pl.ds(x, channels, stride=rows_x), :] = value[:channels]
+            dens[h, 1, pl.ds(x, channels, stride=rows_x), :] = value[channels:]
         left = jnp.concatenate(
             [jnp.concatenate([dens[h, 0], dens[h, 1]], axis=1) for h in range(PAIRED)], axis=0
         ).astype(jnp.bfloat16)
@@ -239,28 +252,60 @@
             value[:, h * LANES : (h + 1) * LANES].reshape(devices, 2 * LANES // devices, LANES)
             for h in range(PAIRED)
         ]
-        sent[:, t] = jnp.concatenate(pieces, axis=1).astype(jnp.bfloat16)
-        out[me, t] = sent[me, t]
-
-        @pl.when(t == 0)
-        def _():
-            pl.semaphore_wait(barrier, grid_x * grid_y - 1)
-
-        for_others(
-            lambda x, y: pltpu.make_async_remote_copy(
-                src_ref=sent.at[x * grid_y + y, t], dst_ref=out.at[me, t],
+        sent[:, slot] = jnp.concatenate(pieces, axis=1).astype(jnp.bfloat16)
+
+    def push(columns, own, first, count=1):
+        for x, y in targets(columns, own):
+            pltpu.make_async_remote_copy(
+                src_ref=sent.at[x * grid_y + y, pl.ds(first, count)],
+                dst_ref=out.at[me, pl.ds(first, count)],
                 send_sem=send_sem, recv_sem=recv_sem,
                 device_id={"gx": x, "gy": y}, device_id_type=MESH,
             ).start()
-        )
-
+
+    def ready(spin):
+        load_spin(spin).wait()
+        if spin == SPINS - 1:
+            for t in range(1, tiles):
+                load(t).start()
+
+    first_products(0, ready)
+    small[0].wait()
+    small[1].wait()
+    weights[...] = folded_weights(jnp.transpose(table[...]), rows[...])
+    second_products(0)
+    small[2].wait()
+    finish(0, 0)
+    pl.semaphore_wait(barrier, grid_x * grid_y - 1)
+    push(urgent, 0, 0)
+    push(lazy, 0, 0)
+    last = tiles - 1
+    for t in range(1, tiles):
+        load(t).wait()
+        if t > 1:
+            finish(t - 1, t - 1)
+        first_products(t)
+        if t > 1:
+            push(urgent, 0, t - 1)
+            if t < last:
+                push(lazy, 0, t - 1)
+            if t == 2:
+                push(near, 0, 0, 2)
+                push([me_y], 1, 0, 2)
+        second_products(t)
+    finish(last, last)
+    push(urgent, 0, last)
+    push(near, 0, 2, tiles - 2)
+    push([me_y], 1, 2, tiles - 2)
+    push(lazy, 0, max(last - 1, 1), last - max(last - 1, 1) + 1)
+    out[me] = sent[me]
     rest = sent.at[pl.ds(0, devices - 1)]
     pltpu.make_async_copy(rest, rest, recv_sem).wait()
     pltpu.make_async_copy(rest, rest, send_sem).wait()
 
 
 def front(prop, gamma_table, devices, grid_y, extent):
-    entries, rows_x, sites = prop.shape
+    rows_x, sites = prop.shape[-2:]
     tiles = sites // (LANES * PAIRED)
     height = 2 * LANES // devices * PAIRED
     channels = gamma_table.shape[0]
@@ -278,8 +323,10 @@
         in_specs=[pl.BlockSpec(memory_space=pltpu.HBM)] * 4,
         out_specs=pl.BlockSpec(memory_space=pltpu.VMEM),
         scratch_shapes=[
-            pltpu.VMEM((tiles, entries, rows_x, PAIRED * LANES), jnp.bfloat16),
-            pltpu.VMEM((PAIRED, (len(ROWS) + PITCH) * rows_x, LANES), jnp.float32),
+            pltpu.VMEM((tiles, *prop.shape[:-1], PAIRED * LANES), jnp.bfloat16),
+            pltpu.VMEM((PAIRED, (len(ROWS) // 2 + PITCH) * rows_x, LANES), jnp.float32),
+            pltpu.VMEM((PAIRED, (len(ROWS) // 2 + PITCH) * rows_x, LANES), jnp.float32),
+            pltpu.VMEM((PAIRED, rows_x, 2 * channels, LANES), jnp.float32),
             pltpu.VMEM((PAIRED, 2, channels * rows_x, LANES), jnp.float32),
             pltpu.VMEM((2 * channels, len(ROWS)), jnp.bfloat16),
             pltpu.VMEM((devices, tiles, height, LANES), jnp.bfloat16),
@@ -287,6 +334,7 @@
             pltpu.VMEM(rows.shape, jnp.int32),
             pltpu.VMEM((2 * LANES, 2 * LANES), jnp.bfloat16),
             pltpu.SemaphoreType.DMA((tiles,)),
+            pltpu.SemaphoreType.DMA((SPINS,)),
             pltpu.SemaphoreType.DMA((3,)),
             pltpu.SemaphoreType.DMA,
             pltpu.SemaphoreType.DMA,
@@ -297,7 +345,7 @@
     )(*pinned)
 
 
-def back_kernel(blocks, along_y, along_x, out, mid):
+def back_kernel(blocks, along_y, along_x, out, mid, result, sem):
     grid_x, _, width = blocks.shape
     channels, local_k, extent, lanes = out.shape
     rows_x = width // channels
@@ -310,20 +358,27 @@
         value = mid[:, g * rows_x : (g + 1) * rows_x, :].reshape(grid_x * rows_x, 2 * cols)
         value = value.astype(jnp.bfloat16)
         stacked = jnp.concatenate([value[:, :cols], value[:, cols:]], axis=0)
-        result = jnp.dot(along_x[...], stacked, preferred_element_type=jnp.float32)
+        spectrum = jnp.dot(along_x[...], stacked, preferred_element_type=jnp.float32)
         for k in range(local_k):
-            out[g, k] = result[:, k * lanes : (k + 1) * lanes]
+            result[g, k] = spectrum[:, k * lanes : (k + 1) * lanes]
+        pltpu.make_async_copy(result.at[g], out.at[g], sem).start()
+    pltpu.make_async_copy(result, out, sem).wait()
 
 
 def back(blocks, channels, extent, local_k):
     grid_x, _, width = blocks.shape
     vmem = pl.BlockSpec(memory_space=pltpu.VMEM)
+    shape = (channels, local_k, extent, 2 * extent)
     return pl.pallas_call(
         back_kernel,
-        out_shape=jax.ShapeDtypeStruct((channels, local_k, extent, 2 * extent), jnp.float32),
+        out_shape=jax.ShapeDtypeStruct(shape, jnp.float32),
         in_specs=[vmem] * 3,
-        out_specs=vmem,
-        scratch_shapes=[pltpu.VMEM((grid_x, width, 4 * local_k * extent), jnp.float32)],
+        out_specs=pl.BlockSpec(memory_space=pl.ANY),
+        scratch_shapes=[
+            pltpu.VMEM((grid_x, width, 4 * local_k * extent), jnp.float32),
+            pltpu.VMEM(shape, jnp.float32),
+            pltpu.SemaphoreType.DMA,
+        ],
         compiler_params=pltpu.CompilerParams(vmem_limit_bytes=24 * 1024 * 1024),
     )(
         blocks,
@@ -341,7 +396,7 @@
     local_k = extent // devices
     results = []
     for t in range(slices):
-        prop = propagator[t].reshape(-1, rows_x, sites)
+        prop = propagator[t].reshape(2, SPINS, -1, rows_x, sites)
         blocks = front(prop, gamma_table, devices, grid_y, extent)
         blocks = blocks.reshape(grid_x, -1, LANES)
         results.append(back(blocks, channels, extent, local_k))

time: 23.6 us -> 20.6 us (0.87)
  Pallas kernels: 23.4 us -> 20.5 us
    pallas_call x1, Pallas kernels: 21.7 us -> 18.9 us  [front(): pl.pallas_call(functools.partial(front_kernel, devices // grid_y, grid_y)...]
where the time goes in v2:
time: 20.6 us; the launch traced here: 20.5 us
  Pallas kernels  20.5 us (100%)
    pallas_call x1, Pallas kernels, front(): pl.pallas_call(functools.partial(front_kernel, devices // grid_y, grid_y)...  18.9 us
    pallas_call x1, Pallas kernels, back(): pl.pallas_call(back_kernel, out_shape=jax.ShapeDtypeStruct(shape, jnp.flo...  1.56 us

profile of v2, /device:TPU:0, one launch (start us, length us, event | category | flops | bytes accessed | tf_op | source)
XLA Modules:
  0.0 20.5 jit_solution(664598442651013697)
XLA Ops:
  0.0 0.0 copy-start.1
  0.0 0.0 copy-start
  0.0 18.9 %shard_map.64 = bf16[32,4,16,128]{3,2,1,0:T(8,128)(2,1)S(1)} custom-call(bf16[2,4,36,8,1024]{4,3,2,1,0:T(8,128)(2,1)} %bitcast.5, s32[8,16]{1,0:T(8,128)} %bitcast.6, s32[8,256]{1,0:T(8,128)} %constant.8.clone.rows_in, bf16[256,256]{1,0:T(8,128)(2,1)} %constant.9.clone.dft_in), custom_call_target="tpu_custom_call" | custom-call | tf_op jit(solution)/shard_map/pallas_call | solution.py:320
  18.9 0.0 copy-done.1
  18.9 0.0 copy-done
  18.9 1.6 %shard_map.65 = f32[16,2,64,128]{3,2,1,0:T(8,128)} custom-call(bf16[8,256,128]{2,1,0:T(8,128)(2,1)S(1)} %bitcast.4, bf16[256,512]{1,0:T(8,128)(2,1)S(1)} %copy-done, bf16[64,128]{1,0:T(8,128)(2,1)S(1)} %copy-done.1), custom_call_target="tpu_custom_call" | custom-call | tf_op jit(solution)/shard_map/pallas_call | solution.py:372
Async XLA Ops:
  0.0 18.9 %copy-start.1 = (bf16[64,128]{1,0:T(8,128)(2,1)S(1)}, bf16[64,128]{1,0:T(8,128)(2,1)}, u32[]{:S(2)}) copy-start(bf16[64,128]{1,0:T(8,128)(2,1)} %constant.11.clone.along_x) | copy-start | bytes 49156
  0.0 18.9 %copy-start = (bf16[256,512]{1,0:T(8,128)(2,1)S(1)}, bf16[256,512]{1,0:T(8,128)(2,1)}, u32[]{:S(2)}) copy-start(bf16[256,512]{1,0:T(8,128)(2,1)} %constant.10.clone.along_y) | copy-start | bytes 786436

commit v3 on v2

--- a/solution.py
+++ b/solution.py
@@ -188,6 +188,7 @@
 
     urgent, lazy = far[: len(far) // 2], far[len(far) // 2 :]
     every = tuple(range(grid_x))
+    early = me_y < grid_y // 2
 
     def targets(columns, own):
         for i in every[own:]:
@@ -213,10 +214,9 @@
         pltpu.make_async_copy(source, target, small_sems.at[n])
         for n, (source, target) in enumerate(((table_in, table), (rows_in, rows), (dft_in, dft)))
     ]
-    load_spin(0).start()
     small[0].start()
     small[1].start()
-    for spin in range(1, SPINS):
+    for spin in range(SPINS):
         load_spin(spin).start()
     small[2].start()
     barrier = pltpu.get_barrier_semaphore()
@@ -269,35 +269,51 @@
             for t in range(1, tiles):
                 load(t).start()
 
-    first_products(0, ready)
     small[0].wait()
     small[1].wait()
     weights[...] = folded_weights(jnp.transpose(table[...]), rows[...])
+    first_products(0, ready)
     second_products(0)
     small[2].wait()
     finish(0, 0)
     pl.semaphore_wait(barrier, grid_x * grid_y - 1)
+    def push_near(first, count):
+        push(near, 0, first, count)
+        push([me_y], 1, first, count)
+
     push(urgent, 0, 0)
     push(lazy, 0, 0)
     last = tiles - 1
+    held = max(last - 1, 1)
     for t in range(1, tiles):
         load(t).wait()
         if t > 1:
             finish(t - 1, t - 1)
         first_products(t)
         if t > 1:
+            if t == held:
+
+                @pl.when(early)
+                def _():
+                    push_near(0, held)
+
             push(urgent, 0, t - 1)
-            if t < last:
+            if t - 1 < held:
                 push(lazy, 0, t - 1)
-            if t == 2:
-                push(near, 0, 0, 2)
-                push([me_y], 1, 0, 2)
         second_products(t)
     finish(last, last)
     push(urgent, 0, last)
-    push(near, 0, 2, tiles - 2)
-    push([me_y], 1, 2, tiles - 2)
-    push(lazy, 0, max(last - 1, 1), last - max(last - 1, 1) + 1)
+
+    @pl.when(early)
+    def _():
+        push_near(held, tiles - held)
+
+    push(lazy, 0, held, tiles - held)
+
+    @pl.when(jnp.logical_not(early))
+    def _():
+        push_near(0, tiles)
+
     out[me] = sent[me]
     rest = sent.at[pl.ds(0, devices - 1)]
     pltpu.make_async_copy(rest, rest, recv_sem).wait()

time: 20.6 us -> 20.4 us (level)
  no operation moved by 1% of the time
where the time goes in v3:
time: 20.4 us; the launch traced here: 20.3 us
  Pallas kernels  20.3 us (100%)
    pallas_call x1, Pallas kernels, front(): pl.pallas_call(functools.partial(front_kernel, devices // grid_y, grid_y)...  18.7 us
    pallas_call x1, Pallas kernels, back(): pl.pallas_call(back_kernel, out_shape=jax.ShapeDtypeStruct(shape, jnp.flo...  1.56 us

profile of v3, /device:TPU:0, one launch (start us, length us, event | category | flops | bytes accessed | tf_op | source)
XLA Modules:
  0.0 20.3 jit_solution(12605651768612600300)
XLA Ops:
  0.0 0.0 copy-start.1
  0.0 0.0 copy-start
  0.0 18.7 %shard_map.64 = bf16[32,4,16,128]{3,2,1,0:T(8,128)(2,1)S(1)} custom-call(bf16[2,4,36,8,1024]{4,3,2,1,0:T(8,128)(2,1)} %bitcast.5, s32[8,16]{1,0:T(8,128)} %bitcast.6, s32[8,256]{1,0:T(8,128)} %constant.8.clone.rows_in, bf16[256,256]{1,0:T(8,128)(2,1)} %constant.9.clone.dft_in), custom_call_target="tpu_custom_call" | custom-call | tf_op jit(solution)/shard_map/pallas_call | solution.py:336
  18.7 0.0 copy-done.1
  18.7 0.0 copy-done
  18.7 1.6 %shard_map.65 = f32[16,2,64,128]{3,2,1,0:T(8,128)} custom-call(bf16[8,256,128]{2,1,0:T(8,128)(2,1)S(1)} %bitcast.4, bf16[256,512]{1,0:T(8,128)(2,1)S(1)} %copy-done, bf16[64,128]{1,0:T(8,128)(2,1)S(1)} %copy-done.1), custom_call_target="tpu_custom_call" | custom-call | tf_op jit(solution)/shard_map/pallas_call | solution.py:388
Async XLA Ops:
  0.0 18.7 %copy-start.1 = (bf16[64,128]{1,0:T(8,128)(2,1)S(1)}, bf16[64,128]{1,0:T(8,128)(2,1)}, u32[]{:S(2)}) copy-start(bf16[64,128]{1,0:T(8,128)(2,1)} %constant.11.clone.along_x) | copy-start | bytes 49156
  0.0 18.7 %copy-start = (bf16[256,512]{1,0:T(8,128)(2,1)S(1)}, bf16[256,512]{1,0:T(8,128)(2,1)}, u32[]{:S(2)}) copy-start(bf16[256,512]{1,0:T(8,128)(2,1)} %constant.10.clone.along_y) | copy-start | bytes 786436
